TPU v7x, 32 devices: a whole 2x2x4 slice. The times are simulated.
32 devices in a mesh: obs: 4 (over y, x), patch: 8 (over z, core).
Axes of the slice: x: 2, y: 2, z: 4, core: 2. Of those that a mesh axis runs over, the one named last changes fastest.
Arguments:
- green: float32 [5120, 5120], P('obs', 'patch'), may hold values from -0.078125 to 0.078125
- data: float32 [5120, 128], P('obs'), may hold values from -6 to 6
- neighbours: int32 [3, 5120], P(None, 'patch'), may hold values from 0 to 5119, as said below
- reg_weight: float32 [128], replicated, may hold values from 0.5 to 2
Outputs:
- slip: float32 [5120, 128], P('patch')
Inputs may be any that keep to these rules, and one draw needn't show every extreme that they name: `neighbours`: entry (k, i) is a patch within 128 of i; an entry equal to i is padding. Distance 128 is reached in every draw.
All inputs are finite; a program needn't handle non-finite values.
Results may differ from a plain program's by a relative error of at most 0.0001.
Values sent between devices are 32-bit elements; how exact they have to be, the bound alone decides.
A program may use at most 64 MiB of HBM per device.

v0:
```python
import functools
import math

import jax
import jax.numpy as jnp
from jax import lax
from jax.experimental import pallas as pl
from jax.experimental.pallas import tpu as pltpu
from jax.sharding import PartitionSpec as P

BAND = 128
ITERS = 3
MESH = pl.DeviceIdType.MESH
F32 = jnp.float32
BF16 = jnp.bfloat16


def dot(a, b):
    return lax.dot_general(a, b, (((1,), (0,)), ((), ())), preferred_element_type=F32)


def split(x):
    hi = x.astype(BF16)
    return hi, (x - hi.astype(F32)).astype(BF16)


def kernel(n_obs, n_patch, nc, bc, green, data, nb, rw, out,
           ghi, glo, gthi, gtlo, lm, lmt, cat_d, cat_r, cat_e,
           d, g, a, wext, slip, sq,
           pf, s, rd, sr, sl, rl, rr, img, bb, br, hal, wr, scs, scr, pls, plr,
           sem_d, sem_l, sem_r, sem_i, sem_b, sem_h, sem_w, sem_s, sem_p, sem_n):
    rows, cols = green.shape
    E = data.shape[1]
    R = rows // 2 // nc
    BR = cols // bc
    CB = cols // BAND
    nz = n_patch // 2
    nbit = n_obs.bit_length() - 1
    obs = lax.axis_index("obs")
    pat = lax.axis_index("patch")
    z = pat // 2
    c = pat % 2
    other = 1 - c
    partner = z * 2 + other
    has_l, has_r = pat > 0, pat < n_patch - 1
    up, down = z < nz - 1, z > 0
    weight = rw[...]

    def at(o, q):
        return (o, q)

    def rcopy(src, dst, sems, dev):
        return pltpu.make_async_remote_copy(
            src_ref=src, dst_ref=dst, send_sem=sems[0], recv_sem=sems[1],
            device_id=dev, device_id_type=MESH)

    def pair(sem, *idx):
        return sem.at[(0,) + idx], sem.at[(1,) + idx]

    barrier = pltpu.get_barrier_semaphore()

    @pl.loop(1, n_patch)
    def _(i):
        pl.semaphore_signal(barrier, inc=1, device_id=at(obs, (pat + i) % n_patch), device_id_type=MESH)

    n_plane = 2 * n_obs

    def plane(i):
        q = (obs * 2 + c + i) % n_plane
        return q // 2, z * 2 + q % 2

    @pl.loop(1, n_plane)
    def _(i):
        pl.semaphore_signal(barrier, inc=1, device_id=plane(i), device_id_type=MESH)

    nblk = rows // BAND

    @pl.loop(0, nblk)
    def _(i):
        r0 = pl.multiple_of(i * BAND, BAND)
        block = green[pl.ds(r0, BAND), :]
        hi, lo = split(block)
        ghi[pl.ds(r0, BAND), :] = hi
        glo[pl.ds(r0, BAND), :] = lo
        hi, lo = split(block.T)
        for j in range(bc):
            gthi[j, :, pl.ds(r0, BAND)] = hi[j * BR:(j + 1) * BR]
            gtlo[j, :, pl.ds(r0, BAND)] = lo[j * BR:(j + 1) * BR]
        hi, lo = split(data[pl.ds(r0, BAND), :])
        cat_r[pl.ds(r0, BAND), 0:E] = hi
        cat_r[pl.ds(r0, BAND), E:2 * E] = lo

    scs[...] = jnp.zeros((ITERS, 8, E), F32)
    zero_c = jnp.zeros((nc, R, E), F32)
    zero_h = jnp.zeros((BAND, E), F32)

    @pl.when(z == 0)
    def _():
        for it in range(ITERS):
            rl[it] = zero_c

    @pl.when(z == nz - 1)
    def _():
        for it in range(ITERS):
            rr[it] = zero_c

    @pl.when(pat == 0)
    def _():
        for it in range(ITERS):
            hal[it, 0] = zero_h
        for it in range(ITERS - 1):
            wr[it, 0] = zero_h

    @pl.when(pat == n_patch - 1)
    def _():
        for it in range(ITERS):
            hal[it, 1] = zero_h
        for it in range(ITERS - 1):
            wr[it, 1] = zero_h

    def build_laplace():
        @pl.loop(0, CB + 2)
        def _(j):
            r0 = pl.multiple_of(j * BAND, BAND)
            col = lax.broadcasted_iota(jnp.int32, (BAND, cols), 0) + j * BAND
            own = lax.broadcasted_iota(jnp.int32, (BAND, cols), 1) + BAND
            m = jnp.where(col == own, 4.0, 0.0)
            col = col + (pat * cols - BAND)
            for k in range(3):
                m = m - jnp.where(col == nb[k:k + 1, :], 1.0, 0.0)
            lmt[pl.ds(r0, BAND), :] = m.astype(BF16)
            lm[:, pl.ds(r0, BAND)] = m.T.astype(BF16)

    pl.semaphore_wait(barrier, n_patch - 1 + n_plane - 1)

    def bit_partner(p, j):
        b0, b1 = 1 << p, 1 << (nbit - 1 - p)
        bit = b0 + (j % 2) * (b1 - b0)
        return at(obs + bit * (1 - 2 * ((obs // bit) % 2)), pat)

    def bcopy(b, p, j):
        return rcopy(bb.at[b, p, j], br.at[b, p, j], pair(sem_b, b, p, j), bit_partner(p, j))

    def backward(b, hook, dst):
        @pl.loop(0, bc)
        def _(j):
            y = dot(gthi[j], cat_r[...])
            bb[b, 0, j] = y[:, :E] + y[:, E:] + dot(gtlo[j], cat_r[:, 0:E])
            bcopy(b, 0, j).start()

        hook()
        for p in range(1, nbit):
            @pl.loop(0, bc)
            def _(j):
                bcopy(b, p - 1, j).wait_recv()
                bb[b, p, j] = bb[b, p - 1, j] + br[b, p - 1, j]
                bcopy(b, p, j).start()

        @pl.loop(0, bc)
        def _(j):
            bcopy(b, nbit - 1, j).wait_recv()
            dst[pl.ds(pl.multiple_of(j * BR, BR), BR), :] = bb[b, nbit - 1, j] + br[b, nbit - 1, j]

        for p in range(nbit):
            @pl.loop(0, bc)
            def _(j):
                bcopy(b, p, j).wait_send()

    def dcopy(it, k):
        return rcopy(pf.at[k], rd.at[it, k], pair(sem_d, it, k), at(obs, partner))

    def rcopy_up(it, src, k):
        return rcopy(src.at[k], rl.at[it, k], pair(sem_l, it, k), at(obs, pat + 2))

    def rcopy_down(it, src, k):
        return rcopy(src.at[k], rr.at[it, k], pair(sem_r, it, k), at(obs, pat - 2))

    def icopy(it, k):
        return rcopy(img.at[it, c, k], img.at[it, c, k], pair(sem_i, it, k), at(obs, partner))

    def put_cat(h, k, value):
        hi, lo = split(value)
        r0 = pl.multiple_of((h * nc + k) * R, R)
        cat_r[pl.ds(r0, R), 0:E] = hi
        cat_r[pl.ds(r0, R), E:2 * E] = lo

    def hcopy_r(it):
        return rcopy(d.at[pl.ds(cols - BAND, BAND)], hal.at[it, 0], pair(sem_h, it, 0), at(obs, pat + 1))

    def hcopy_l(it):
        return rcopy(d.at[pl.ds(0, BAND)], hal.at[it, 1], pair(sem_h, it, 1), at(obs, pat - 1))

    def forward(it, hook):
        last = it == ITERS - 1

        @pl.when(has_r)
        def _():
            hcopy_r(it).start()

        @pl.when(has_l)
        def _():
            hcopy_l(it).start()

        hi, lo = split(d[...])
        cat_d[:, 0:E] = hi
        cat_d[:, E:2 * E] = lo

        def part(h, k):
            r0 = pl.multiple_of((h * nc + k) * R, R)
            y = dot(ghi[pl.ds(r0, R), :], cat_d[...])
            return y[:, :E] + y[:, E:] + dot(glo[pl.ds(r0, R), :], cat_d[:, 0:E])

        @pl.loop(0, nc)
        def _(k):
            pf[k] = part(other, k)
            dcopy(it, k).start()

        @pl.loop(0, nc)
        def _(k):
            y = part(c, k)
            dcopy(it, k).wait_recv()
            s[k] = y + rd[it, k]

            @pl.when(z == 0)
            def _():
                rcopy_up(it, s, k).start()

            @pl.when(z == nz - 1)
            def _():
                rcopy_down(it, s, k).start()

        def chain(t):
            kl = t - z
            kr = t - (nz - 1 - z)
            kt = t - jnp.maximum(z, nz - 1 - z)

            @pl.when(down & (kl >= 0) & (kl < nc))
            def _():
                rcopy_up(it, sr, kl).wait_recv()

                @pl.when(up)
                def _():
                    sr[kl] = rl[it, kl] + s[kl]
                    rcopy_up(it, sr, kl).start()

            @pl.when(up & (kr >= 0) & (kr < nc))
            def _():
                rcopy_down(it, sl, kr).wait_recv()

                @pl.when(down)
                def _():
                    sl[kr] = rr[it, kr] + s[kr]
                    rcopy_down(it, sl, kr).start()

            @pl.when((kt >= 0) & (kt < nc))
            def _():
                total = rl[it, kt] + s[kt] + rr[it, kt]
                if last:
                    sq[...] += jnp.sum((total * total).reshape(R // 8, 8, E), axis=0)
                else:
                    img[it, c, kt] = total
                    icopy(it, kt).start()
                    put_cat(c, kt, total)

        if last:
            sq[...] = jnp.zeros((8, E), F32)
            hook()
        pl.loop(1, nc + nz - 1)(chain)

        if not last:
            @pl.loop(0, nc)
            def _(k):
                icopy(it, k).wait_recv()
                put_cat(other, k, img[it, other, k])

        @pl.loop(0, nc)
        def _(k):
            dcopy(it, k).wait_send()
            if not last:
                icopy(it, k).wait_send()

            @pl.when(up)
            def _():
                rcopy_up(it, sr, k).wait_send()

            @pl.when(down)
            def _():
                rcopy_down(it, sl, k).wait_send()

    def laplace(it):
        @pl.when(has_l)
        def _():
            hcopy_r(it).wait_recv()

        @pl.when(has_r)
        def _():
            hcopy_l(it).wait_recv()

        for r0, n, v in ((0, BAND, hal[it, 0]), (BAND, cols, d[...]), (BAND + cols, BAND, hal[it, 1])):
            hi, lo = split(v)
            cat_e[r0:r0 + n, 0:E] = hi
            cat_e[r0:r0 + n, E:2 * E] = lo

        @pl.when(has_r)
        def _():
            hcopy_r(it).wait_send()

        @pl.when(has_l)
        def _():
            hcopy_l(it).wait_send()

    def lap_rows(i):
        r0 = pl.multiple_of(i * BAND, BAND)
        y = dot(lm[pl.ds(r0, BAND), :], cat_e[...])
        return r0, weight * (y[:, :E] + y[:, E:])

    def wcopy_l(it):
        return rcopy(wext.at[pl.ds(0, BAND)], wr.at[it, 1], pair(sem_w, it, 1), at(obs, pat - 1))

    def wcopy_r(it):
        return rcopy(wext.at[pl.ds(BAND + cols, BAND)], wr.at[it, 0], pair(sem_w, it, 0), at(obs, pat + 1))

    def reg_start(it):
        laplace(it)

        @pl.loop(0, CB)
        def _(i):
            r0, u = lap_rows(i)
            hi, lo = split(u)
            cat_d[pl.ds(r0, BAND), 0:E] = hi
            cat_d[pl.ds(r0, BAND), E:2 * E] = lo

        @pl.loop(0, CB + 2)
        def _(i):
            r0 = pl.multiple_of(i * BAND, BAND)
            y = dot(lmt[pl.ds(r0, BAND), :], cat_d[...])
            wext[pl.ds(r0, BAND), :] = weight * (y[:, :E] + y[:, E:])

        @pl.when(has_l)
        def _():
            wcopy_l(it).start()

        @pl.when(has_r)
        def _():
            wcopy_r(it).start()

    def reg_end(it):
        a[...] += wext[BAND:BAND + cols, :]

        @pl.when(has_l)
        def _():
            wcopy_r(it).wait_recv()

        @pl.when(has_r)
        def _():
            wcopy_l(it).wait_recv()

        a[0:BAND, :] += wr[it, 0]
        a[cols - BAND:cols, :] += wr[it, 1]

        @pl.when(has_l)
        def _():
            wcopy_l(it).wait_send()

        @pl.when(has_r)
        def _():
            wcopy_r(it).wait_send()

    def scopy(it, slot, q):
        return rcopy(scs.at[it], scr.at[it, slot], (sem_s.at[0, it, q], sem_s.at[1, it, slot]), at(obs, q))

    def sums_start(it):
        scr[it, pat] = scs[it]

        @pl.loop(1, n_patch)
        def _(i):
            scopy(it, pat, (pat + i) % n_patch).start()

    def sums_end(it):
        @pl.loop(1, n_patch)
        def _(i):
            q = (pat + i) % n_patch
            scopy(it, q, q).wait_recv()

        @pl.loop(1, n_patch)
        def _(i):
            q = (pat + i) % n_patch
            scopy(it, pat, q).wait_send()

        return jnp.sum(scr[it], axis=0)

    def pcopy(slot, i):
        o, q = plane(i)
        return rcopy(pls, plr.at[slot], (sem_p.at[i], sem_n.at[slot]), (o, q))

    def rowsum(x):
        return jnp.sum(x, axis=0, keepdims=True)

    backward(0, build_laplace, g)
    d[...] = g[...]
    norm = None
    for it in range(ITERS - 1):
        forward(it, None)
        backward(it + 1, functools.partial(reg_start, it), a)
        reg_end(it)
        gv, dv, av = g[...], d[...], a[...]
        scs[it, 0:1, :] = rowsum(gv * gv)
        scs[it, 1:2, :] = rowsum(dv * av)
        scs[it, 2:3, :] = rowsum(gv * av)
        scs[it, 3:4, :] = rowsum(av * av)
        sums_start(it)
        tot = sums_end(it)
        if norm is None:
            norm = tot[0:1]
        step = norm / tot[1:2]
        after = norm - 2.0 * step * tot[2:3] + step * step * tot[3:4]
        if it == 0:
            slip[...] = step * d[...]
        else:
            slip[...] += step * d[...]
        g[...] = g[...] - step * a[...]
        d[...] = g[...] + (after / norm) * d[...]
        norm = after

    last = ITERS - 1

    def reg_norm():
        laplace(last)
        scs[last] = jnp.zeros((8, E), F32)

        @pl.loop(0, CB)
        def _(i):
            _, u = lap_rows(i)
            scs[last] += jnp.sum((u * u).reshape(BAND // 8, 8, E), axis=0)

        sums_start(last)

    forward(last, reg_norm)
    me = obs * 2 + c
    pls[...] = sq[...]
    plr[me] = sq[...]

    @pl.loop(1, n_plane)
    def _(i):
        pcopy(me, i).start()

    reg = rowsum(sums_end(last))

    @pl.loop(1, n_plane)
    def _(i):
        pcopy((me + i) % n_plane, i).wait_recv()

    curvature = rowsum(jnp.sum(plr[...], axis=0)) + reg
    out[...] = slip[...] + (norm / curvature) * d[...]

    @pl.loop(1, n_plane)
    def _(i):
        pcopy(me, i).wait_send()


def shards(green, data, neighbours, reg_weight):
    rows, cols = green.shape
    E = data.shape[1]
    n_obs, n_patch = lax.axis_size("obs"), lax.axis_size("patch")
    nbit = n_obs.bit_length() - 1
    nc = rows // 2 // 128
    bc = 4
    R, BR, ext = rows // 2 // nc, cols // bc, cols + 2 * BAND
    V = pltpu.VMEM
    D = pltpu.SemaphoreType.DMA
    scratch = [
        V((rows, cols), BF16), V((rows, cols), BF16),
        V((bc, BR, rows), BF16), V((bc, BR, rows), BF16),
        V((cols, ext), BF16), V((ext, cols), BF16),
        V((cols, 2 * E), BF16), V((rows, 2 * E), BF16), V((ext, 2 * E), BF16),
        V((cols, E), F32), V((cols, E), F32), V((cols, E), F32), V((ext, E), F32), V((cols, E), F32),
        V((8, E), F32),
        V((nc, R, E), F32), V((nc, R, E), F32), V((ITERS, nc, R, E), F32),
        V((nc, R, E), F32), V((nc, R, E), F32),
        V((ITERS, nc, R, E), F32), V((ITERS, nc, R, E), F32),
        V((ITERS - 1, 2, nc, R, E), F32),
        V((ITERS, nbit, bc, BR, E), F32), V((ITERS, nbit, bc, BR, E), F32),
        V((ITERS, 2, BAND, E), F32), V((ITERS - 1, 2, BAND, E), F32),
        V((ITERS, 8, E), F32), V((ITERS, n_patch, 8, E), F32),
        V((8, E), F32), V((2 * n_obs, 8, E), F32),
        D((2, ITERS, nc)), D((2, ITERS, nc)), D((2, ITERS, nc)), D((2, ITERS - 1, nc)),
        D((2, ITERS, nbit, bc)), D((2, ITERS, 2)), D((2, ITERS - 1, 2)),
        D((2, ITERS, n_patch)), D((2 * n_obs,)), D((2 * n_obs,)),
    ]
    return pl.pallas_call(
        functools.partial(kernel, n_obs, n_patch, nc, bc),
        out_shape=jax.ShapeDtypeStruct((cols, E), F32),
        in_specs=[pl.BlockSpec(memory_space=pltpu.VMEM)] * 4,
        out_specs=pl.BlockSpec(memory_space=pltpu.VMEM),
        scratch_shapes=scratch,
        compiler_params=pltpu.CompilerParams(
            collective_id=0, has_side_effects=True, vmem_limit_bytes=56 * 1024 * 1024),
    )(green, data, neighbours, reg_weight.reshape(1, E))


def solution(mesh):
    in_specs = (P("obs", "patch"), P("obs", None), P(None, "patch"), P())
    return jax.shard_map(shards, mesh=mesh, in_specs=in_specs, out_specs=P("patch", None), check_vma=False)
```

profile of v0, /device:TPU:0, one launch (start us, length us, event | category | flops | bytes accessed | tf_op | source)
XLA Modules:
  0.0 121.0 jit_solution(5805382695273684795)
XLA Ops:
  0.0 119.3 %shard_map.46 = f32[640,128]{1,0:T(8,128)} custom-call(f32[1280,640]{1,0:T(8,128)} %green.1, f32[1280,128]{1,0:T(8,128)} %data.1, s32[3,640]{1,0:T(4,128)} %nb.1, f32[1,128]{1,0:T(1,128)} %bitcast.1), custom_call_target="tpu_custom_call" | custom-call | tf_op jit(solution)/shard_map/pallas_call | solution.py:490
  119.3 1.7 %copy.6 = f32[640,128]{1,0:T(8,128)} copy(f32[640,128]{1,0:T(8,128)} %shard_map.46) | data formatting | bytes 655360
where the time goes:
time: 121 us
  Pallas kernels  119 us (98%)
  local copies, waits for them, and re-layouts  1.72 us (1%)
    pallas_call x1, Pallas kernels, shards(): pl.pallas_call(functools.partial(kernel, n_obs, n_patch, nc, bc), out_sha...  119 us

commit v1 on v0

--- a/solution.py
+++ b/solution.py
@@ -26,13 +26,16 @@
 
 def kernel(n_obs, n_patch, nc, bc, green, data, nb, rw, out,
            ghi, glo, gthi, gtlo, lm, lmt, cat_d, cat_r, cat_e,
-           d, g, a, wext, slip, sq,
+           d, g, a, wext, slip, sq, hd, hg, qd, qg,
            pf, s, rd, sr, sl, rl, rr, img, bb, br, hal, wr, scs, scr, pls, plr,
            sem_d, sem_l, sem_r, sem_i, sem_b, sem_h, sem_w, sem_s, sem_p, sem_n):
     rows, cols = green.shape
     E = data.shape[1]
     R = rows // 2 // nc
     BR = cols // bc
+    half = rows // 2
+    per = 4
+    lag = 4
     CB = cols // BAND
     nz = n_patch // 2
     nbit = n_obs.bit_length() - 1
@@ -83,9 +86,8 @@
         ghi[pl.ds(r0, BAND), :] = hi
         glo[pl.ds(r0, BAND), :] = lo
         hi, lo = split(block.T)
-        for j in range(bc):
-            gthi[j, :, pl.ds(r0, BAND)] = hi[j * BR:(j + 1) * BR]
-            gtlo[j, :, pl.ds(r0, BAND)] = lo[j * BR:(j + 1) * BR]
+        gthi[:, pl.ds(r0, BAND)] = hi
+        gtlo[:, pl.ds(r0, BAND)] = lo
         hi, lo = split(data[pl.ds(r0, BAND), :])
         cat_r[pl.ds(r0, BAND), 0:E] = hi
         cat_r[pl.ds(r0, BAND), E:2 * E] = lo
@@ -142,11 +144,12 @@
         return rcopy(bb.at[b, p, j], br.at[b, p, j], pair(sem_b, b, p, j), bit_partner(p, j))
 
     def backward(b, hook, dst):
-        @pl.loop(0, bc)
-        def _(j):
-            y = dot(gthi[j], cat_r[...])
-            bb[b, 0, j] = y[:, :E] + y[:, E:] + dot(gtlo[j], cat_r[:, 0:E])
-            bcopy(b, 0, j).start()
+        for m in range(0, bc, per):
+            y = dot(gthi[m * BR:(m + per) * BR, :], cat_r[...])
+            y = y[:, :E] + y[:, E:] + dot(gtlo[m * BR:(m + per) * BR, :], cat_r[:, 0:E])
+            bb[b, 0, m:m + per] = y.reshape(per, BR, E)
+            for j in range(m, m + per):
+                bcopy(b, 0, j).start()
 
         hook()
         for p in range(1, nbit):
@@ -185,12 +188,12 @@
         cat_r[pl.ds(r0, R), E:2 * E] = lo
 
     def hcopy_r(it):
-        return rcopy(d.at[pl.ds(cols - BAND, BAND)], hal.at[it, 0], pair(sem_h, it, 0), at(obs, pat + 1))
+        return rcopy((a if it else g).at[pl.ds(cols - BAND, BAND)], hal.at[it, 0], pair(sem_h, it, 0), at(obs, pat + 1))
 
     def hcopy_l(it):
-        return rcopy(d.at[pl.ds(0, BAND)], hal.at[it, 1], pair(sem_h, it, 1), at(obs, pat - 1))
-
-    def forward(it, hook):
+        return rcopy((a if it else g).at[pl.ds(0, BAND)], hal.at[it, 1], pair(sem_h, it, 1), at(obs, pat - 1))
+
+    def forward(it, sums, hook):
         last = it == ITERS - 1
 
         @pl.when(has_r)
@@ -201,25 +204,29 @@
         def _():
             hcopy_l(it).start()
 
-        hi, lo = split(d[...])
+        hi, lo = split((a if it else g)[...])
         cat_d[:, 0:E] = hi
         cat_d[:, E:2 * E] = lo
-
-        def part(h, k):
-            r0 = pl.multiple_of((h * nc + k) * R, R)
-            y = dot(ghi[pl.ds(r0, R), :], cat_d[...])
-            return y[:, :E] + y[:, E:] + dot(glo[pl.ds(r0, R), :], cat_d[:, 0:E])
+        sums()
+
+        def part(h):
+            r0 = pl.multiple_of(h * half, half)
+            y = dot(ghi[pl.ds(r0, half), :], cat_d[...])
+            y = y[:, :E] + y[:, E:] + dot(glo[pl.ds(r0, half), :], cat_d[:, 0:E])
+            return y.reshape(nc, R, E)
+
+        pf[...] = part(other)
 
         @pl.loop(0, nc)
         def _(k):
-            pf[k] = part(other, k)
             dcopy(it, k).start()
+
+        s[...] = part(c)
 
         @pl.loop(0, nc)
         def _(k):
-            y = part(c, k)
             dcopy(it, k).wait_recv()
-            s[k] = y + rd[it, k]
+            s[k] += rd[it, k]
 
             @pl.when(z == 0)
             def _():
@@ -229,10 +236,10 @@
             def _():
                 rcopy_down(it, s, k).start()
 
-        def chain(t):
-            kl = t - z
-            kr = t - (nz - 1 - z)
-            kt = t - jnp.maximum(z, nz - 1 - z)
+        def chain(t, ends=True):
+            kl = t - lag * z
+            kr = t - lag * (nz - 1 - z)
+            kt = t - lag * jnp.maximum(z, nz - 1 - z)
 
             @pl.when(down & (kl >= 0) & (kl < nc))
             def _():
@@ -252,9 +259,19 @@
                     sl[kr] = rr[it, kr] + s[kr]
                     rcopy_down(it, sl, kr).start()
 
+            if not ends:
+                return
+
             @pl.when((kt >= 0) & (kt < nc))
             def _():
                 total = rl[it, kt] + s[kt] + rr[it, kt]
+                if it:
+                    step, ratio = scalars
+                    rest = qg[kt] - step * total
+                    total = rest + ratio * qd[kt]
+                if not last:
+                    qg[kt] = rest if it else total
+                    qd[kt] = total
                 if last:
                     sq[...] += jnp.sum((total * total).reshape(R // 8, 8, E), axis=0)
                 else:
@@ -264,8 +281,9 @@
 
         if last:
             sq[...] = jnp.zeros((8, E), F32)
-            hook()
-        pl.loop(1, nc + nz - 1)(chain)
+        pl.loop(lag, lag * (nz // 2))(functools.partial(chain, ends=False))
+        scalars = hook()
+        pl.loop(lag * (nz // 2), nc + lag * (nz - 1))(chain)
 
         if not last:
             @pl.loop(0, nc)
@@ -287,7 +305,7 @@
             def _():
                 rcopy_down(it, sl, k).wait_send()
 
-    def laplace(it):
+    def halo_wait(it):
         @pl.when(has_l)
         def _():
             hcopy_r(it).wait_recv()
@@ -296,18 +314,19 @@
         def _():
             hcopy_l(it).wait_recv()
 
-        for r0, n, v in ((0, BAND, hal[it, 0]), (BAND, cols, d[...]), (BAND + cols, BAND, hal[it, 1])):
+        @pl.when(has_r)
+        def _():
+            hcopy_r(it).wait_send()
+
+        @pl.when(has_l)
+        def _():
+            hcopy_l(it).wait_send()
+
+    def laplace():
+        for r0, n, v in ((0, BAND, hd[0]), (BAND, cols, d[...]), (BAND + cols, BAND, hd[1])):
             hi, lo = split(v)
             cat_e[r0:r0 + n, 0:E] = hi
             cat_e[r0:r0 + n, E:2 * E] = lo
-
-        @pl.when(has_r)
-        def _():
-            hcopy_r(it).wait_send()
-
-        @pl.when(has_l)
-        def _():
-            hcopy_l(it).wait_send()
 
     def lap_rows(i):
         r0 = pl.multiple_of(i * BAND, BAND)
@@ -321,7 +340,7 @@
         return rcopy(wext.at[pl.ds(BAND + cols, BAND)], wr.at[it, 0], pair(sem_w, it, 0), at(obs, pat + 1))
 
     def reg_start(it):
-        laplace(it)
+        laplace()
 
         @pl.loop(0, CB)
         def _(i):
@@ -396,46 +415,59 @@
     def rowsum(x):
         return jnp.sum(x, axis=0, keepdims=True)
 
-    backward(0, build_laplace, g)
-    d[...] = g[...]
-    norm = None
-    for it in range(ITERS - 1):
-        forward(it, None)
-        backward(it + 1, functools.partial(reg_start, it), a)
-        reg_end(it)
+    norms = []
+
+    def dots(it):
         gv, dv, av = g[...], d[...], a[...]
         scs[it, 0:1, :] = rowsum(gv * gv)
         scs[it, 1:2, :] = rowsum(dv * av)
         scs[it, 2:3, :] = rowsum(gv * av)
         scs[it, 3:4, :] = rowsum(av * av)
         sums_start(it)
-        tot = sums_end(it)
-        if norm is None:
-            norm = tot[0:1]
+
+    def first():
+        halo_wait(0)
+        hg[...] = hal[0]
+        hd[...] = hal[0]
+
+    def advance(it):
+        tot = sums_end(it - 1)
+        if it == 1:
+            norms.append(tot[0:1])
+        norm = norms[-1]
         step = norm / tot[1:2]
         after = norm - 2.0 * step * tot[2:3] + step * step * tot[3:4]
-        if it == 0:
+        ratio = after / norm
+        norms.append(after)
+        halo_wait(it)
+        if it == 1:
             slip[...] = step * d[...]
         else:
             slip[...] += step * d[...]
         g[...] = g[...] - step * a[...]
-        d[...] = g[...] + (after / norm) * d[...]
-        norm = after
-
+        d[...] = g[...] + ratio * d[...]
+        hg[...] = hg[...] - step * hal[it]
+        hd[...] = hg[...] + ratio * hd[...]
+        if it == ITERS - 1:
+            laplace()
+
+            @pl.loop(0, CB)
+            def _(i):
+                _, u = lap_rows(i)
+                scs[it] += jnp.sum((u * u).reshape(BAND // 8, 8, E), axis=0)
+
+            sums_start(it)
+        return step, ratio
+
+    backward(0, build_laplace, g)
+    d[...] = g[...]
+    forward(0, lambda: None, first)
+    for it in range(1, ITERS):
+        backward(it, functools.partial(reg_start, it - 1), a)
+        reg_end(it - 1)
+        forward(it, functools.partial(dots, it - 1), functools.partial(advance, it))
     last = ITERS - 1
-
-    def reg_norm():
-        laplace(last)
-        scs[last] = jnp.zeros((8, E), F32)
-
-        @pl.loop(0, CB)
-        def _(i):
-            _, u = lap_rows(i)
-            scs[last] += jnp.sum((u * u).reshape(BAND // 8, 8, E), axis=0)
-
-        sums_start(last)
-
-    forward(last, reg_norm)
+    norm = norms[-1]
     me = obs * 2 + c
     pls[...] = sq[...]
     plr[me] = sq[...]
@@ -463,18 +495,19 @@
     E = data.shape[1]
     n_obs, n_patch = lax.axis_size("obs"), lax.axis_size("patch")
     nbit = n_obs.bit_length() - 1
-    nc = rows // 2 // 128
-    bc = 4
+    nc = rows // 2 // 64
+    bc = 8
     R, BR, ext = rows // 2 // nc, cols // bc, cols + 2 * BAND
     V = pltpu.VMEM
     D = pltpu.SemaphoreType.DMA
     scratch = [
         V((rows, cols), BF16), V((rows, cols), BF16),
-        V((bc, BR, rows), BF16), V((bc, BR, rows), BF16),
+        V((cols, rows), BF16), V((cols, rows), BF16),
         V((cols, ext), BF16), V((ext, cols), BF16),
         V((cols, 2 * E), BF16), V((rows, 2 * E), BF16), V((ext, 2 * E), BF16),
         V((cols, E), F32), V((cols, E), F32), V((cols, E), F32), V((ext, E), F32), V((cols, E), F32),
         V((8, E), F32),
+        V((2, BAND, E), F32), V((2, BAND, E), F32), V((nc, R, E), F32), V((nc, R, E), F32),
         V((nc, R, E), F32), V((nc, R, E), F32), V((ITERS, nc, R, E), F32),
         V((nc, R, E), F32), V((nc, R, E), F32),
         V((ITERS, nc, R, E), F32), V((ITERS, nc, R, E), F32),

time: 121 us -> 103 us (0.85)
  Pallas kernels: 119 us -> 101 us
    pallas_call x1, Pallas kernels: 119 us -> 101 us  [shards(): pl.pallas_call(functools.partial(kernel, n_obs, n_patch, nc, bc), out_sha...]
where the time goes in v1:
time: 103 us
  Pallas kernels  101 us (98%)
  local copies, waits for them, and re-layouts  1.72 us (2%)
    pallas_call x1, Pallas kernels, shards(): pl.pallas_call(functools.partial(kernel, n_obs, n_patch, nc, bc), out_sha...  101 us

profile of v1, /device:TPU:0, one launch (start us, length us, event | category | flops | bytes accessed | tf_op | source)
XLA Modules:
  0.0 102.8 jit_solution(14333820264376346066)
XLA Ops:
  0.0 101.1 %shard_map.46 = f32[640,128]{1,0:T(8,128)} custom-call(f32[1280,640]{1,0:T(8,128)} %green.1, f32[1280,128]{1,0:T(8,128)} %data.1, s32[3,640]{1,0:T(4,128)} %nb.1, f32[1,128]{1,0:T(1,128)} %bitcast.1), custom_call_target="tpu_custom_call" | custom-call | tf_op jit(solution)/shard_map/pallas_call | solution.py:523
  101.1 1.7 %copy.6 = f32[640,128]{1,0:T(8,128)} copy(f32[640,128]{1,0:T(8,128)} %shard_map.46) | data formatting | bytes 655360
